TPU v7x, 32 devices: a whole 2x2x4 slice. The times are simulated.
32 devices in a mesh: ep: 4 (over y, core), fs: 8 (over z, x).
Axes of the slice: x: 2, y: 2, z: 4, core: 2. Of those that a mesh axis runs over, the one named last changes fastest.
Arguments:
- grads: bfloat16 [4, 4, 128, 14336], P('ep', None, 'fs'), may hold values from -64 to 64
- counts: int32 [4, 4], replicated, may hold values from 16 to 2047
- weight: bfloat16 [4, 128, 14336], P('ep', 'fs'), may hold values from -3 to 3
- mom: float32 [4, 128, 14336], P('ep', 'fs'), may hold values from -64 to 64
- second: float32 [4, 128, 14336], P('ep', 'fs'), may hold values from 0.1 to 10
- in_weight: float32 [6, 32], replicated, may hold values from -2.5 to 2.5
- in_bias: float32 [32], replicated, may hold values from -3 to 3
- out_weight: float32 [32, 2], replicated, may hold values from -1 to 1
- out_bias: float32 [2], replicated, may hold values from -3 to 3
Outputs:
- new_weight: bfloat16 [4, 128, 14336], P('ep')
- new_mom: float32 [4, 128, 14336], P('ep', 'fs')
- new_second: float32 [4, 128, 14336], P('ep', 'fs')
All inputs are finite; a program needn't handle non-finite values.
Results may differ from a plain program's by a relative error of at most 0.0019.
Values may be sent and summed in bfloat16 or wider, within the bound.
A program may use at most 64 MiB of HBM per device.

v0:
```python
import jax
import jax.numpy as jnp
from jax import lax
from jax.sharding import PartitionSpec as P

MOMENTUM_DECAY = 0.9
SECOND_DECAY = 0.99
NORM_EPS = 1e-06
ROOT_EPS = 1e-08
STEP_SCALE = 0.2
EXP_SCALE = 0.5


def learned_step(
    gradient,
    mom_next,
    second_next,
    weight,
    grad_norm,
    mom_norm,
    in_weight,
    in_bias,
    out_weight,
    out_bias,
):
    inv_root = lax.rsqrt(second_next + ROOT_EPS)
    features = jnp.stack(
        [
            gradient / grad_norm,
            mom_next / mom_norm,
            mom_next * inv_root,
            gradient * inv_root,
            weight.astype(jnp.float32),
            jnp.broadcast_to(jnp.log(mom_norm), gradient.shape),
        ]
    )
    hidden = jax.nn.relu(
        jnp.einsum("fh,fab->hab", in_weight, features, precision=lax.Precision.HIGHEST)
        + in_bias[:, None, None]
    )
    outputs = (
        jnp.einsum("hk,hab->kab", out_weight, hidden, precision=lax.Precision.HIGHEST)
        + out_bias[:, None, None]
    )
    update = STEP_SCALE * outputs[0] * jnp.exp(EXP_SCALE * outputs[1])
    return (weight.astype(jnp.float32) - update).astype(jnp.bfloat16)


def add_sources(arrived):
    return jnp.sum(arrived.astype(jnp.float32), axis=0)


def per_device(grads, counts, weight, mom, second, in_weight, in_bias, out_weight, out_bias):
    source = lax.axis_index("ep")
    counts_f = counts.astype(jnp.float32)
    totals = jnp.sum(counts_f, axis=0)
    share_row = lax.dynamic_index_in_dim(counts_f, source, 0, keepdims=False) / totals
    weighted = share_row[None, :, None, None] * grads.astype(jnp.float32)
    outgoing = weighted.astype(jnp.bfloat16)
    gradient = add_sources(lax.all_to_all(outgoing, "ep", split_axis=1, concat_axis=0, tiled=True))[
        0
    ]
    mom_here = mom[0]
    second_here = second[0]
    mom_next = MOMENTUM_DECAY * mom_here + (1.0 - MOMENTUM_DECAY) * gradient
    second_next = SECOND_DECAY * second_here + (1.0 - SECOND_DECAY) * gradient * gradient
    entries = gradient.shape[0] * gradient.shape[1] * lax.axis_size("fs")
    grad_sq, mom_sq = lax.psum((jnp.sum(gradient * gradient), jnp.sum(mom_next * mom_next)), "fs")
    grad_norm = jnp.sqrt(grad_sq / entries + NORM_EPS)
    mom_norm = jnp.sqrt(mom_sq / entries + NORM_EPS)
    width = gradient.shape[1]

    def block_step(items):
        grad_block, mom_block, second_block, weight_block = items
        return learned_step(
            grad_block,
            mom_block,
            second_block,
            weight_block,
            grad_norm,
            mom_norm,
            in_weight,
            in_bias,
            out_weight,
            out_bias,
        )

    blocks = lax.map(
        block_step,
        (
            gradient.reshape(-1, 2, width),
            mom_next.reshape(-1, 2, width),
            second_next.reshape(-1, 2, width),
            weight[0].reshape(-1, 2, width),
        ),
    )
    updated = blocks.reshape(gradient.shape)
    gathered = lax.all_gather(updated[None], "fs", axis=1, tiled=True)
    return (gathered, mom_next[None], second_next[None])


def solution(mesh):
    in_specs = (
        P("ep", None, "fs", None),
        P(),
        P("ep", "fs", None),
        P("ep", "fs", None),
        P("ep", "fs", None),
        P(),
        P(),
        P(),
        P(),
    )
    out_specs = (P("ep", None, None), P("ep", "fs", None), P("ep", "fs", None))
    return jax.shard_map(
        per_device, mesh=mesh, in_specs=in_specs, out_specs=out_specs, check_vma=False
    )
```

profile of v0, /device:TPU:0, one launch (start us, length us, event | category | flops | bytes accessed | tf_op | source)
XLA Modules:
  0.0 230.4 jit_solution(16413111683950979025)
XLA Ops:
  8.6 3.1 %multiply_convert_fusion = bf16[1,4,16,14336]{3,2,0,1:T(8,128)(2,1)} fusion(bf16[1,4,16,14336]{3,2,1,0:T(8,128)(2,1)} %param.11, f32[4]{0:T(128)S(1)} %bitcast_divide_fusion), kind=kLoop, calls=%fused_computation.22 | loop fusion | flops 2752512 | bytes 3670032 | tf_op jit(solution)/shard_map/convert_element_type | solution.py:59
  11.7 4.3 %all-to-all-start = ((bf16[1,4,16,14336]{3,2,0,1:T(8,128)(2,1)}), bf16[1,4,16,14336]{3,2,0,1:T(8,128)(2,1)S(1)}, u32[]{:S(2)}, u32[]{:S(2)}) async-start(bf16[1,4,16,14336]{3,2,0,1:T(8,128)(2,1)} %multiply_convert_fusion), calls=%async_computation | async-start | bytes 3670016 | tf_op jit(solution)/shard_map/all_to_all | solution.py:60
  16.3 22.5 %all-to-all-done = bf16[1,4,16,14336]{3,2,0,1:T(8,128)(2,1)S(1)} async-done(((bf16[1,4,16,14336]{3,2,0,1:T(8,128)(2,1)}), bf16[1,4,16,14336]{3,2,0,1:T(8,128)(2,1)S(1)}, u32[]{:S(2)}, u32[]{:S(2)}) %all-to-all-start) | async-done | bytes 1835040 | tf_op jit(solution)/shard_map/all_to_all | solution.py:60
  42.6 23.1 %all-reduce = (f32[]{:T(128)}, f32[]{:T(128)}) all-reduce(f32[]{:T(128)} %get-tuple-element.159, f32[]{:T(128)} %get-tuple-element.158), channel_id=1, replica_groups=mesh['ep'=4,'fs'=8] {'fs'}, use_global_device_ids=true, to_apply=%region_3.4 | all-reduce | flops 2 | bytes 16 | tf_op jit(solution)/shard_map/psum | solution.py:68
  66.5 3.0 %fusion.10 = (f32[1,16,14336]{2,1,0:T(8,128)}, f32[1,16,14336]{2,1,0:T(8,128)S(1)}, f32[1,16,14336]{2,1,0:T(8,128)}, f32[1,16,14336]{2,1,0:T(8,128)S(1)}) fusion(f32[16,14336]{1,0:T(8,128)S(1)} %convert_reduce_fusion, f32[1,16,14336]{2,1,0:T(8,128)} %param.15, f32[1,16,14336]{2,1,0:T(8,128)} %param.14), kind=kLoop, calls=%fused_computation.26 | loop fusion | flops 1605632 | bytes 6422528 | tf_op jit(solution)/shard_map/add | solution.py:66
  72.2 4.1 %fusion.9 = (f32[8,2,14336]{2,0,1:T(8,128)S(1)}, f32[8,2,14336]{2,0,1:T(8,128)}, f32[8,2,14336]{2,0,1:T(8,128)}) fusion(f32[8,2,14336]{2,1,0:T(2,128)S(1)} %mul.131, f32[8,2,14336]{2,1,0:T(2,128)S(1)} %copy-done, f32[8,2,14336]{2,1,0:T(2,128)} %mul.122), kind=kLoop, calls=%fused_computation.25 | loop fusion | flops 1146880 | bytes 5505024 | tf_op jit(solution)/shard_map/add | solution.py:66
  76.3 78.5 %while.11 = (s32[]{:T(128)}, bf16[8,2,14336]{2,1,0:T(2,128)(2,1)}, bf16[8,2,14336]{2,1,0:T(2,128)(2,1)S(1)}, f32[8,2,14336]{2,0,1:T(8,128)}, f32[]{:T(128)}, /*i...) while((s32[]{:T(128)}, bf16[8,2,14336]{2,1,0:T(2,128)(2,1)}, ...), condition=%wide.region_7.8_spmd, body=%wide.region_6.7_spmd.sunk | while | flops 90316800 | bytes 18638680 | solution.py:88
  76.3 2.2 dynamic-slice_multiply_fusion.3
  79.9 3.2 %fusion.27 = f32[32,2,14336]{2,0,1:T(8,128)S(1)} fusion(f32[6,2,14336]{2,0,1:T(8,128)S(1)} %stack.4, f32[32]{0:T(128)S(1)} %get-tuple-element.324, f32[6,32]{1,0:T(8,128)S(1)} %get-tuple-element.323), kind=kOutput, calls=%fused_computation.2.clone.1 | convolution fusion | flops 67895296 | bytes 4359040 | tf_op jit(solution)/shard_map/while/body/eval_jaxpr/fh,fab->hab/dot_general | solution.py:38
  86.2 2.2 dynamic-slice_multiply_fusion.3
  89.7 3.2 %fusion.27 = f32[32,2,14336]{2,0,1:T(8,128)S(1)} fusion(f32[6,2,14336]{2,0,1:T(8,128)S(1)} %stack.4, f32[32]{0:T(128)S(1)} %get-tuple-element.324, f32[6,32]{1,0:T(8,128)S(1)} %get-tuple-element.323), kind=kOutput, calls=%fused_computation.2.clone.1 | convolution fusion | flops 67895296 | bytes 4359040 | tf_op jit(solution)/shard_map/while/body/eval_jaxpr/fh,fab->hab/dot_general | solution.py:38
  96.0 2.2 dynamic-slice_multiply_fusion.3
  99.5 3.2 %fusion.27 = f32[32,2,14336]{2,0,1:T(8,128)S(1)} fusion(f32[6,2,14336]{2,0,1:T(8,128)S(1)} %stack.4, f32[32]{0:T(128)S(1)} %get-tuple-element.324, f32[6,32]{1,0:T(8,128)S(1)} %get-tuple-element.323), kind=kOutput, calls=%fused_computation.2.clone.1 | convolution fusion | flops 67895296 | bytes 4359040 | tf_op jit(solution)/shard_map/while/body/eval_jaxpr/fh,fab->hab/dot_general | solution.py:38
  105.8 2.2 dynamic-slice_multiply_fusion.3
  109.3 3.2 %fusion.27 = f32[32,2,14336]{2,0,1:T(8,128)S(1)} fusion(f32[6,2,14336]{2,0,1:T(8,128)S(1)} %stack.4, f32[32]{0:T(128)S(1)} %get-tuple-element.324, f32[6,32]{1,0:T(8,128)S(1)} %get-tuple-element.323), kind=kOutput, calls=%fused_computation.2.clone.1 | convolution fusion | flops 67895296 | bytes 4359040 | tf_op jit(solution)/shard_map/while/body/eval_jaxpr/fh,fab->hab/dot_general | solution.py:38
  115.6 2.2 dynamic-slice_multiply_fusion.3
  119.1 3.2 %fusion.27 = f32[32,2,14336]{2,0,1:T(8,128)S(1)} fusion(f32[6,2,14336]{2,0,1:T(8,128)S(1)} %stack.4, f32[32]{0:T(128)S(1)} %get-tuple-element.324, f32[6,32]{1,0:T(8,128)S(1)} %get-tuple-element.323), kind=kOutput, calls=%fused_computation.2.clone.1 | convolution fusion | flops 67895296 | bytes 4359040 | tf_op jit(solution)/shard_map/while/body/eval_jaxpr/fh,fab->hab/dot_general | solution.py:38
  128.9 3.2 %fusion.27 = f32[32,2,14336]{2,0,1:T(8,128)S(1)} fusion(f32[6,2,14336]{2,0,1:T(8,128)S(1)} %stack.4, f32[32]{0:T(128)S(1)} %get-tuple-element.324, f32[6,32]{1,0:T(8,128)S(1)} %get-tuple-element.323), kind=kOutput, calls=%fused_computation.2.clone.1 | convolution fusion | flops 67895296 | bytes 4359040 | tf_op jit(solution)/shard_map/while/body/eval_jaxpr/fh,fab->hab/dot_general | solution.py:38
  135.2 2.2 dynamic-slice_multiply_fusion.3
  138.7 3.2 %fusion.27 = f32[32,2,14336]{2,0,1:T(8,128)S(1)} fusion(f32[6,2,14336]{2,0,1:T(8,128)S(1)} %stack.4, f32[32]{0:T(128)S(1)} %get-tuple-element.324, f32[6,32]{1,0:T(8,128)S(1)} %get-tuple-element.323), kind=kOutput, calls=%fused_computation.2.clone.1 | convolution fusion | flops 67895296 | bytes 4359040 | tf_op jit(solution)/shard_map/while/body/eval_jaxpr/fh,fab->hab/dot_general | solution.py:38
  145.0 2.2 dynamic-slice_multiply_fusion.3
  148.5 3.2 %fusion.27 = f32[32,2,14336]{2,0,1:T(8,128)S(1)} fusion(f32[6,2,14336]{2,0,1:T(8,128)S(1)} %stack.4, f32[32]{0:T(128)S(1)} %get-tuple-element.324, f32[6,32]{1,0:T(8,128)S(1)} %get-tuple-element.323), kind=kOutput, calls=%fused_computation.2.clone.1 | convolution fusion | flops 67895296 | bytes 4359040 | tf_op jit(solution)/shard_map/while/body/eval_jaxpr/fh,fab->hab/dot_general | solution.py:38
  156.8 62.5 %all-gather.2.cloned.1.call-done = bf16[1,128,14336]{2,1,0:T(8,128)(2,1)} async-done(((bf16[1,16,14336]{2,1,0:T(8,128)(2,1)}), bf16[1,128,14336]{2,1,0:T(8,128)(2,1)}) %all-gather.2.cloned.1.call-update) | async-done | bytes 3670032 | tf_op jit(solution)/shard_map/all_gather | solution.py:98
  219.3 4.2 %copy.64 = bf16[1,128,14336]{2,1,0:T(8,128)(2,1)} copy(bf16[1,128,14336]{2,1,0:T(8,128)(2,1)} %all-gather.2.cloned.1.call-done) | data formatting | bytes 7340032
  (114 shorter events, 46.7 us)
Async XLA Ops:
  8.6 7.4 %copy-start.3 = (bf16[1,16,14336]{2,1,0:T(8,128)(2,1)S(1)}, bf16[1,16,14336]{2,1,0:T(8,128)(2,1)}, u32[]{:S(2)}) copy-start(bf16[1,16,14336]{2,1,0:T(8,128)(2,1)} %param.13) | copy-start | bytes 1376260
  11.7 27.1 %all-to-all-start = ((bf16[1,4,16,14336]{3,2,0,1:T(8,128)(2,1)}), bf16[1,4,16,14336]{3,2,0,1:T(8,128)(2,1)S(1)}, u32[]{:S(2)}, u32[]{:S(2)}) async-start(bf16[1,4,16,14336]{3,2,0,1:T(8,128)(2,1)} %multiply_convert_fusion), calls=%async_computation | async-start | bytes 3670016 | tf_op jit(solution)/shard_map/all_to_all | solution.py:60
  16.0 203.3 %all-gather.2.cloned.1.call-start = ((), (), s32[]{:S(2)}) async-start(), calls=%async_computation.1 | async-start | bytes 4128768 | tf_op jit(solution)/shard_map/all_gather | solution.py:98
  69.4 2.8 %copy-start = (f32[8,2,14336]{2,1,0:T(2,128)S(1)}, f32[8,2,14336]{2,1,0:T(2,128)}, u32[]{:S(2)}) copy-start(f32[8,2,14336]{2,1,0:T(2,128)} %reshape_squeeze.7) | copy-start | bytes 2752516
  70.9 5.4 %copy-start.4 = (f32[6,32]{1,0:T(8,128)S(1)}, f32[6,32]{1,0:T(8,128)}, u32[]{:S(2)}) copy-start(f32[6,32]{1,0:T(8,128)} %param.16) | copy-start | bytes 2308
  70.9 5.4 %copy-start.5 = (f32[32,2]{0,1:T(2,128)S(1)}, f32[32,2]{0,1:T(2,128)}, u32[]{:S(2)}) copy-start(f32[32,2]{0,1:T(2,128)} %param.18) | copy-start | bytes 772
  70.9 5.4 %copy-start.6 = (f32[32]{0:T(128)S(1)}, f32[32]{0:T(128)}, u32[]{:S(2)}) copy-start(f32[32]{0:T(128)} %param.17) | copy-start | bytes 388
  70.9 5.4 %copy-start.7 = (f32[2]{0:T(128)S(1)}, f32[2]{0:T(128)}, u32[]{:S(2)}) copy-start(f32[2]{0:T(128)} %param.19) | copy-start | bytes 28
  76.3 2.2 copy-start.1
  83.1 3.1 %copy-start.2 = (f32[8,2,14336]{2,0,1:T(8,128)S(1)}, f32[8,2,14336]{2,0,1:T(8,128)}, u32[]{:S(2)}) copy-start(f32[8,2,14336]{2,0,1:T(8,128)} %copy-done.1) | copy-start | bytes 2752516 | tf_op jit(solution)/shard_map/while
  86.2 2.2 copy-start.1
  92.9 3.1 %copy-start.2 = (f32[8,2,14336]{2,0,1:T(8,128)S(1)}, f32[8,2,14336]{2,0,1:T(8,128)}, u32[]{:S(2)}) copy-start(f32[8,2,14336]{2,0,1:T(8,128)} %copy-done.1) | copy-start | bytes 2752516 | tf_op jit(solution)/shard_map/while
  96.0 2.2 copy-start.1
  102.7 3.1 %copy-start.2 = (f32[8,2,14336]{2,0,1:T(8,128)S(1)}, f32[8,2,14336]{2,0,1:T(8,128)}, u32[]{:S(2)}) copy-start(f32[8,2,14336]{2,0,1:T(8,128)} %copy-done.1) | copy-start | bytes 2752516 | tf_op jit(solution)/shard_map/while
  105.8 2.2 copy-start.1
  112.5 3.1 %copy-start.2 = (f32[8,2,14336]{2,0,1:T(8,128)S(1)}, f32[8,2,14336]{2,0,1:T(8,128)}, u32[]{:S(2)}) copy-start(f32[8,2,14336]{2,0,1:T(8,128)} %copy-done.1) | copy-start | bytes 2752516 | tf_op jit(solution)/shard_map/while
  115.6 2.2 copy-start.1
  122.3 3.1 %copy-start.2 = (f32[8,2,14336]{2,0,1:T(8,128)S(1)}, f32[8,2,14336]{2,0,1:T(8,128)}, u32[]{:S(2)}) copy-start(f32[8,2,14336]{2,0,1:T(8,128)} %copy-done.1) | copy-start | bytes 2752516 | tf_op jit(solution)/shard_map/while
  125.4 2.2 copy-start.1
  132.1 3.1 %copy-start.2 = (f32[8,2,14336]{2,0,1:T(8,128)S(1)}, f32[8,2,14336]{2,0,1:T(8,128)}, u32[]{:S(2)}) copy-start(f32[8,2,14336]{2,0,1:T(8,128)} %copy-done.1) | copy-start | bytes 2752516 | tf_op jit(solution)/shard_map/while
  135.2 2.2 copy-start.1
  141.9 3.1 %copy-start.2 = (f32[8,2,14336]{2,0,1:T(8,128)S(1)}, f32[8,2,14336]{2,0,1:T(8,128)}, u32[]{:S(2)}) copy-start(f32[8,2,14336]{2,0,1:T(8,128)} %copy-done.1) | copy-start | bytes 2752516 | tf_op jit(solution)/shard_map/while
  145.0 2.2 copy-start.1
  151.8 3.1 %copy-start.2 = (f32[8,2,14336]{2,0,1:T(8,128)S(1)}, f32[8,2,14336]{2,0,1:T(8,128)}, u32[]{:S(2)}) copy-start(f32[8,2,14336]{2,0,1:T(8,128)} %copy-done.1) | copy-start | bytes 2752516 | tf_op jit(solution)/shard_map/while
Sparse Core Ops, SparseCore 0:
  156.9 62.3 all-gather.1
where the time goes:
time: 231 us; the launch traced here: 230 us
  waiting for transfers between devices  85.1 us (37%)
  matrix products  42 us (18%)
  other arithmetic  34.4 us (15%)
  local copies, waits for them, and re-layouts  25.4 us (11%)
  blocking collectives  23.1 us (10%)
  between operations  15.5 us (7%)
  starting transfers between devices  4.27 us (2%)
    all_gather x1, waiting for transfers between devices, per_device(): gathered = lax.all_gather(updated[None], 'fs', axis=1, tiled=True)  62.5 us
    dot_general x8, matrix products, learned_step(): jnp.einsum('fh,fab->hab', in_weight, features, precision=lax.Precision.HI...  25.6 us
    psum x1, blocking collectives, per_device(): lax.psum((jnp.sum(gradient * gradient), jnp.sum(mom_next * mom_next)), 'fs')  23.1 us
    all_to_all x1, waiting for transfers between devices, per_device(): lax.all_to_all(outgoing, 'ep', split_axis=1, concat_axis=0, tiled=True)  22.5 us
    mul x8, other arithmetic, learned_step(): gradient * inv_root  17.3 us
    dot_general x8, matrix products, learned_step(): jnp.einsum('hk,hab->kab', out_weight, hidden, precision=lax.Precision.HIG...  16.4 us
    another operation x8, local copies, waits for them, and re-layouts, learned_step(): jnp.stack([gradient / grad_norm, mom_next / mom_norm, mom_next * inv_root...  8.98 us
    add x2, other arithmetic, per_device(): SECOND_DECAY * second_here + (1.0 - SECOND_DECAY) * gradient * gradient  7.04 us
  transfers between devices with their start and end apart: 2, of which 2 were waited for; matrix products, arithmetic and copies ran while one was open for 0% of the time, Pallas kernels for 0%

commit v1 on v0

--- a/solution.py
+++ b/solution.py
@@ -1,3 +1,4 @@
+import functools
 import jax
 import jax.numpy as jnp
 from jax import lax
@@ -9,6 +10,23 @@
 ROOT_EPS = 1e-08
 STEP_SCALE = 0.2
 EXP_SCALE = 0.5
+
+
+def fix_the_cards(chunk, ndim_at):
+    v_now = lax.axis_size("fs")
+    opened = lax.axis_index("fs")
+    right_arr, w_next = (v_now, opened)
+    h_now, val2 = (chunk, 1)
+    while val2 < right_arr:
+        earlier = lax.ppermute(h_now, "fs", [(dev_i, dev_i ^ val2) for dev_i in range(right_arr)])
+        current_value = jnp.concatenate([h_now, earlier], ndim_at)
+        after = jnp.concatenate([earlier, h_now], ndim_at)
+        h_now = jnp.where(w_next & val2 == 0, current_value, after)
+        val2 = 2 * val2
+    return h_now
+
+
+_perform_lanes = functools.partial(fix_the_cards, ndim_at=1)
 
 
 def learned_step(
@@ -95,7 +113,7 @@
         ),
     )
     updated = blocks.reshape(gradient.shape)
-    gathered = lax.all_gather(updated[None], "fs", axis=1, tiled=True)
+    gathered = _perform_lanes(updated[None])
     return (gathered, mom_next[None], second_next[None])
 
 

time: 231 us -> 259 us (1.12)
  waiting for transfers between devices: 85.1 us -> 123 us
  between operations: 15.5 us -> 2.22 us
  other arithmetic: 34.4 us -> 40.3 us
  local copies, waits for them, and re-layouts: 25.4 us -> 22.1 us
    ppermute x0 -> x3, waiting for transfers between devices: none -> 101 us  [fix_the_cards(): lax.ppermute(h_now, 'fs', [(dev_i, dev_i ^ val2) for dev_i in range(right...]
    all_gather x1 -> x0, waiting for transfers between devices: 62.5 us -> none  [per_device(): gathered = lax.all_gather(updated[None], 'fs', axis=1, tiled=True)]
    dynamic_slice x8, local copies, waits for them, and re-layouts: 0.4 us -> 6.93 us  [per_device(): lax.map(block_step, (gradient.reshape(-1, 2, width), mom_next.reshape(-1,...]
    select_n x0 -> x4, other arithmetic: none -> 5.62 us  [fix_the_cards(): h_now = jnp.where(w_next & val2 == 0, current_value, after)]
    dynamic_update_slice x8, local copies, waits for them, and re-layouts: 5.49 us -> 0.62 us  [per_device(): lax.map(block_step, (gradient.reshape(-1, 2, width), mom_next.reshape(-1,...]
    unnamed x13 -> x12, local copies, waits for them, and re-layouts: 4.22 us -> 0.02 us
  transfers between devices with their start and end apart: 2 -> 4, of which waited for: 2 -> 4; matrix products, arithmetic and copies ran while one was open for 0% -> 1% of each run, Pallas kernels for 0% -> 0%
where the time goes in v1:
time: 259 us; the launch traced here: 258 us
  waiting for transfers between devices  123 us (47%)
  matrix products  42 us (16%)
  other arithmetic  40.3 us (16%)
  blocking collectives  23.1 us (9%)
  local copies, waits for them, and re-layouts  22.1 us (9%)
  starting transfers between devices  4.41 us (2%)
    ppermute x3, waiting for transfers between devices, fix_the_cards(): lax.ppermute(h_now, 'fs', [(dev_i, dev_i ^ val2) for dev_i in range(right...  101 us
    dot_general x8, matrix products, learned_step(): jnp.einsum('fh,fab->hab', in_weight, features, precision=lax.Precision.HI...  25.6 us
    psum x1, blocking collectives, per_device(): lax.psum((jnp.sum(gradient * gradient), jnp.sum(mom_next * mom_next)), 'fs')  23.1 us
    all_to_all x1, waiting for transfers between devices, per_device(): lax.all_to_all(outgoing, 'ep', split_axis=1, concat_axis=0, tiled=True)  21.8 us
    mul x8, other arithmetic, learned_step(): gradient * inv_root  17.4 us
    dot_general x8, matrix products, learned_step(): jnp.einsum('hk,hab->kab', out_weight, hidden, precision=lax.Precision.HIG...  16.4 us
    another operation x8, local copies, waits for them, and re-layouts, learned_step(): jnp.stack([gradient / grad_norm, mom_next / mom_norm, mom_next * inv_root...  8.98 us
    add x2, other arithmetic, per_device(): SECOND_DECAY * second_here + (1.0 - SECOND_DECAY) * gradient * gradient  7.04 us
  transfers between devices with their start and end apart: 4, of which 4 were waited for; matrix products, arithmetic and copies ran while one was open for 1% of the time, Pallas kernels for 0%

profile of v1, /device:TPU:0, one launch (start us, length us, event | category | flops | bytes accessed | tf_op | source)
XLA Modules:
  0.0 257.6 jit_solution(111634860547315002)
XLA Ops:
  2.0 3.1 %multiply_convert_fusion = bf16[1,4,16,14336]{3,2,0,1:T(8,128)(2,1)} fusion(bf16[1,4,16,14336]{3,2,1,0:T(8,128)(2,1)} %param.11, f32[4]{0:T(128)S(1)} %bitcast_divide_fusion), kind=kLoop, calls=%fused_computation.23 | loop fusion | flops 2752512 | bytes 3670032 | tf_op jit(solution)/shard_map/convert_element_type | solution.py:77
  5.2 4.3 %all-to-all-start = ((bf16[1,4,16,14336]{3,2,0,1:T(8,128)(2,1)}), bf16[1,4,16,14336]{3,2,0,1:T(8,128)(2,1)S(1)}, u32[]{:S(2)}, u32[]{:S(2)}) async-start(bf16[1,4,16,14336]{3,2,0,1:T(8,128)(2,1)} %multiply_convert_fusion), calls=%async_computation | async-start | bytes 3670016 | tf_op jit(solution)/shard_map/all_to_all | solution.py:78
  10.6 21.8 %all-to-all-done = bf16[1,4,16,14336]{3,2,0,1:T(8,128)(2,1)S(1)} async-done(((bf16[1,4,16,14336]{3,2,0,1:T(8,128)(2,1)}), bf16[1,4,16,14336]{3,2,0,1:T(8,128)(2,1)S(1)}, u32[]{:S(2)}, u32[]{:S(2)}) %all-to-all-start) | async-done | bytes 1835040 | tf_op jit(solution)/shard_map/all_to_all | solution.py:78
  36.1 23.1 %all-reduce = (f32[]{:T(128)}, f32[]{:T(128)}) all-reduce(f32[]{:T(128)} %get-tuple-element.159, f32[]{:T(128)} %get-tuple-element.158), channel_id=1, replica_groups=mesh['ep'=4,'fs'=8] {'fs'}, use_global_device_ids=true, to_apply=%region_3.4 | all-reduce | flops 2 | bytes 16 | tf_op jit(solution)/shard_map/psum | solution.py:86
  59.9 3.0 %fusion.11 = (f32[1,16,14336]{2,1,0:T(8,128)}, f32[1,16,14336]{2,1,0:T(8,128)S(1)}, f32[1,16,14336]{2,1,0:T(8,128)}, f32[1,16,14336]{2,1,0:T(8,128)S(1)}) fusion(f32[16,14336]{1,0:T(8,128)S(1)} %convert_reduce_fusion, f32[1,16,14336]{2,1,0:T(8,128)} %param.15, f32[1,16,14336]{2,1,0:T(8,128)} %param.14), kind=kLoop, calls=%fused_computation.30 | loop fusion | flops 1605632 | bytes 6422528 | tf_op jit(solution)/shard_map/add | solution.py:84
  65.7 4.1 %fusion.10 = (f32[8,2,14336]{2,0,1:T(8,128)S(1)}, f32[8,2,14336]{2,0,1:T(8,128)}, f32[8,2,14336]{2,0,1:T(8,128)}) fusion(f32[8,2,14336]{2,1,0:T(2,128)S(1)} %mul.131, f32[8,2,14336]{2,1,0:T(2,128)S(1)} %copy-done, f32[8,2,14336]{2,1,0:T(2,128)} %mul.122), kind=kLoop, calls=%fused_computation.29 | loop fusion | flops 1146880 | bytes 5505024 | tf_op jit(solution)/shard_map/add | solution.py:84
  69.8 80.4 %while.11 = (s32[]{:T(128)}, bf16[8,2,14336]{2,1,0:T(2,128)(2,1)S(1)}, bf16[8,2,14336]{2,1,0:T(2,128)(2,1)}, f32[8,2,14336]{2,0,1:T(8,128)}, f32[]{:T(128)}, /*i...) while((s32[]{:T(128)}, ...), condition=%wide.region_7.8_spmd, body=%wide.region_6.7_spmd.sunk | while | flops 90316800 | bytes 18695516 | solution.py:106
  74.2 3.2 %fusion.28 = f32[32,2,14336]{2,0,1:T(8,128)S(1)} fusion(f32[6,2,14336]{2,0,1:T(8,128)S(1)} %stack.4, f32[32]{0:T(128)S(1)} %get-tuple-element.324, f32[6,32]{1,0:T(8,128)S(1)} %get-tuple-element.323), kind=kOutput, calls=%fused_computation.2.clone.1 | convolution fusion | flops 67895296 | bytes 4359040 | tf_op jit(solution)/shard_map/while/body/eval_jaxpr/fh,fab->hab/dot_general | solution.py:56
  79.8 2.2 dynamic-slice_multiply_fusion.3
  84.2 3.2 %fusion.28 = f32[32,2,14336]{2,0,1:T(8,128)S(1)} fusion(f32[6,2,14336]{2,0,1:T(8,128)S(1)} %stack.4, f32[32]{0:T(128)S(1)} %get-tuple-element.324, f32[6,32]{1,0:T(8,128)S(1)} %get-tuple-element.323), kind=kOutput, calls=%fused_computation.2.clone.1 | convolution fusion | flops 67895296 | bytes 4359040 | tf_op jit(solution)/shard_map/while/body/eval_jaxpr/fh,fab->hab/dot_general | solution.py:56
  89.9 2.2 dynamic-slice_multiply_fusion.3
  94.2 3.2 %fusion.28 = f32[32,2,14336]{2,0,1:T(8,128)S(1)} fusion(f32[6,2,14336]{2,0,1:T(8,128)S(1)} %stack.4, f32[32]{0:T(128)S(1)} %get-tuple-element.324, f32[6,32]{1,0:T(8,128)S(1)} %get-tuple-element.323), kind=kOutput, calls=%fused_computation.2.clone.1 | convolution fusion | flops 67895296 | bytes 4359040 | tf_op jit(solution)/shard_map/while/body/eval_jaxpr/fh,fab->hab/dot_general | solution.py:56
  99.9 2.2 dynamic-slice_multiply_fusion.3
  104.3 3.2 %fusion.28 = f32[32,2,14336]{2,0,1:T(8,128)S(1)} fusion(f32[6,2,14336]{2,0,1:T(8,128)S(1)} %stack.4, f32[32]{0:T(128)S(1)} %get-tuple-element.324, f32[6,32]{1,0:T(8,128)S(1)} %get-tuple-element.323), kind=kOutput, calls=%fused_computation.2.clone.1 | convolution fusion | flops 67895296 | bytes 4359040 | tf_op jit(solution)/shard_map/while/body/eval_jaxpr/fh,fab->hab/dot_general | solution.py:56
  110.0 2.2 dynamic-slice_multiply_fusion.3
  114.3 3.2 %fusion.28 = f32[32,2,14336]{2,0,1:T(8,128)S(1)} fusion(f32[6,2,14336]{2,0,1:T(8,128)S(1)} %stack.4, f32[32]{0:T(128)S(1)} %get-tuple-element.324, f32[6,32]{1,0:T(8,128)S(1)} %get-tuple-element.323), kind=kOutput, calls=%fused_computation.2.clone.1 | convolution fusion | flops 67895296 | bytes 4359040 | tf_op jit(solution)/shard_map/while/body/eval_jaxpr/fh,fab->hab/dot_general | solution.py:56
  120.0 2.2 dynamic-slice_multiply_fusion.3
  124.4 3.2 %fusion.28 = f32[32,2,14336]{2,0,1:T(8,128)S(1)} fusion(f32[6,2,14336]{2,0,1:T(8,128)S(1)} %stack.4, f32[32]{0:T(128)S(1)} %get-tuple-element.324, f32[6,32]{1,0:T(8,128)S(1)} %get-tuple-element.323), kind=kOutput, calls=%fused_computation.2.clone.1 | convolution fusion | flops 67895296 | bytes 4359040 | tf_op jit(solution)/shard_map/while/body/eval_jaxpr/fh,fab->hab/dot_general | solution.py:56
  134.4 3.2 %fusion.28 = f32[32,2,14336]{2,0,1:T(8,128)S(1)} fusion(f32[6,2,14336]{2,0,1:T(8,128)S(1)} %stack.4, f32[32]{0:T(128)S(1)} %get-tuple-element.324, f32[6,32]{1,0:T(8,128)S(1)} %get-tuple-element.323), kind=kOutput, calls=%fused_computation.2.clone.1 | convolution fusion | flops 67895296 | bytes 4359040 | tf_op jit(solution)/shard_map/while/body/eval_jaxpr/fh,fab->hab/dot_general | solution.py:56
  144.5 3.2 %fusion.28 = f32[32,2,14336]{2,0,1:T(8,128)S(1)} fusion(f32[6,2,14336]{2,0,1:T(8,128)S(1)} %stack.4, f32[32]{0:T(128)S(1)} %get-tuple-element.324, f32[6,32]{1,0:T(8,128)S(1)} %get-tuple-element.323), kind=kOutput, calls=%fused_computation.2.clone.1 | convolution fusion | flops 67895296 | bytes 4359040 | tf_op jit(solution)/shard_map/while/body/eval_jaxpr/fh,fab->hab/dot_general | solution.py:56
  150.6 8.3 %collective-permute-done = bf16[1,16,14336]{2,1,0:T(8,128)(2,1)S(1)} collective-permute-done((bf16[1,16,14336]{2,1,0:T(8,128)(2,1)S(1)}, bf16[1,16,14336]{2,1,0:T(8,128)(2,1)S(1)}, u32[]{:S(2)}, u32[]{:S(2)}) %collective-permute-start) | collective-permute-done | bytes 458784 | tf_op jit(solution)/shard_map/ppermute | solution.py:21
  159.3 16.8 %collective-permute-done.1 = bf16[1,32,14336]{2,1,0:T(8,128)(2,1)S(1)} collective-permute-done((bf16[1,32,14336]{2,1,0:T(8,128)(2,1)S(1)}, bf16[1,32,14336]{2,1,0:T(8,128)(2,1)S(1)}, u32[]{:S(2)}, u32[]{:S(2)}) %collective-permute-start.1) | collective-permute-done | bytes 917536 | tf_op jit(solution)/shard_map/ppermute | solution.py:21
  178.0 75.8 %collective-permute-done.2 = bf16[1,64,14336]{2,1,0:T(8,128)(2,1)} collective-permute-done((bf16[1,64,14336]{2,1,0:T(8,128)(2,1)}, bf16[1,64,14336]{2,1,0:T(8,128)(2,1)}, u32[]{:S(2)}, u32[]{:S(2)}) %collective-permute-start.2) | collective-permute-done | bytes 1835040 | tf_op jit(solution)/shard_map/ppermute | solution.py:21
  253.8 3.8 %maximum_select_fusion = bf16[1,128,14336]{2,1,0:T(8,128)(2,1)} fusion(bf16[1,64,14336]{2,1,0:T(8,128)(2,1)} %collective-permute-done.2, bf16[1,64,14336]{2,1,0:T(8,128)(2,1)S(1)} %fusion.9, pred[]{:T(512)S(6)} %eq.9), kind=kLoop, calls=%fused_computation.21 | loop fusion | flops 16515072 | bytes 7340033 | tf_op jit(solution)/shard_map/jit(_where)/select_n | solution.py:24
  (122 shorter events, 54.2 us)
Async XLA Ops:
  2.0 7.4 %copy-start.3 = (bf16[1,16,14336]{2,1,0:T(8,128)(2,1)S(1)}, bf16[1,16,14336]{2,1,0:T(8,128)(2,1)}, u32[]{:S(2)}) copy-start(bf16[1,16,14336]{2,1,0:T(8,128)(2,1)} %param.13) | copy-start | bytes 1376260
  5.2 27.1 %all-to-all-start = ((bf16[1,4,16,14336]{3,2,0,1:T(8,128)(2,1)}), bf16[1,4,16,14336]{3,2,0,1:T(8,128)(2,1)S(1)}, u32[]{:S(2)}, u32[]{:S(2)}) async-start(bf16[1,4,16,14336]{3,2,0,1:T(8,128)(2,1)} %multiply_convert_fusion), calls=%async_computation | async-start | bytes 3670016 | tf_op jit(solution)/shard_map/all_to_all | solution.py:78
  62.9 2.8 %copy-start = (f32[8,2,14336]{2,1,0:T(2,128)S(1)}, f32[8,2,14336]{2,1,0:T(2,128)}, u32[]{:S(2)}) copy-start(f32[8,2,14336]{2,1,0:T(2,128)} %reshape_squeeze.7) | copy-start | bytes 2752516
  64.4 5.4 %copy-start.4 = (f32[6,32]{1,0:T(8,128)S(1)}, f32[6,32]{1,0:T(8,128)}, u32[]{:S(2)}) copy-start(f32[6,32]{1,0:T(8,128)} %param.16) | copy-start | bytes 2308
  64.4 5.4 %copy-start.5 = (f32[32,2]{0,1:T(2,128)S(1)}, f32[32,2]{0,1:T(2,128)}, u32[]{:S(2)}) copy-start(f32[32,2]{0,1:T(2,128)} %param.18) | copy-start | bytes 772
  64.4 5.4 %copy-start.6 = (f32[32]{0:T(128)S(1)}, f32[32]{0:T(128)}, u32[]{:S(2)}) copy-start(f32[32]{0:T(128)} %param.17) | copy-start | bytes 388
  64.4 5.4 %copy-start.7 = (f32[2]{0:T(128)S(1)}, f32[2]{0:T(128)}, u32[]{:S(2)}) copy-start(f32[2]{0:T(128)} %param.19) | copy-start | bytes 28
  69.8 2.2 copy-start.1
  77.4 2.5 copy-start.2
  79.8 2.2 copy-start.1
  87.4 2.5 copy-start.2
  89.9 2.2 copy-start.1
  97.5 2.5 copy-start.2
  99.9 2.2 copy-start.1
  107.5 2.5 copy-start.2
  110.0 2.2 copy-start.1
  117.6 2.5 copy-start.2
  120.0 2.2 copy-start.1
  127.6 2.5 copy-start.2
  137.6 2.5 copy-start.2
  147.7 2.5 copy-start.2
  150.4 8.5 %collective-permute-start = (bf16[1,16,14336]{2,1,0:T(8,128)(2,1)S(1)}, bf16[1,16,14336]{2,1,0:T(8,128)(2,1)S(1)}, u32[]{:S(2)}, u32[]{:S(2)}) collective-permute-start(bf16[1,16,14336]{2,1,0:T(8,128)(2,1)S(1)} %broadcast_in_dim_reshape.3), channel_id=1, source_target_pairs={{0,1},{1,0},{2,3},{3,2},{4,5},{5,4},{6,7},{7,6},{8,9},{9,8},{10,11... | collective-permute-start | bytes 1376264 | tf_op jit(solution)/shard_map/ppermute | solution.py:21
  159.1 17.1 %collective-permute-start.1 = (bf16[1,32,14336]{2,1,0:T(8,128)(2,1)S(1)}, bf16[1,32,14336]{2,1,0:T(8,128)(2,1)S(1)}, u32[]{:S(2)}, u32[]{:S(2)}) collective-permute-start(bf16[1,32,14336]{2,1,0:T(8,128)(2,1)S(1)} %maximum_select_fusion.4), channel_id=1, source_target_pairs={{0,2},{1,3},{2,0},{3,1},{4,6},{5,7},{6,4},{7,5},{8,10},{9,11},{10,... | collective-permute-start | bytes 2752520 | tf_op jit(solution)/shard_map/ppermute | solution.py:21
  177.7 76.1 %collective-permute-start.2 = (bf16[1,64,14336]{2,1,0:T(8,128)(2,1)}, bf16[1,64,14336]{2,1,0:T(8,128)(2,1)}, u32[]{:S(2)}, u32[]{:S(2)}) collective-permute-start(bf16[1,64,14336]{2,1,0:T(8,128)(2,1)} %maximum_select_fusion.2), channel_id=1, source_target_pairs={{0,4},{1,5},{2,6},{3,7},{4,0},{5,1},{6,2},{7,3},{8,12},{9,13},{10,... | collective-permute-start | bytes 5505032 | tf_op jit(solution)/shard_map/ppermute | solution.py:21
  (2 other events, 4.4 us)
